TPU v7x, 32 devices: a whole 2x2x4 slice. The times are simulated.
32 devices in a mesh: rows: 4 (over z), tp: 4 (over y, x), unit: 2 (over core).
Axes of the slice: x: 2, y: 2, z: 4, core: 2. Of those that a mesh axis runs over, the one named last changes fastest.
Arguments:
- w_query: bfloat16 [5120, 4096], P(('unit', 'rows'), 'tp'), parts along dimension 0, may hold values from -0.125 to 0.125
- low_query: bfloat16 [5120, 64], P(('unit', 'rows')), parts along dimension 0, may hold values from -0.125 to 0.125
- high_query: bfloat16 [128, 4096], P('unit', 'tp'), parts along dimension 0, may hold values from -0.75 to 0.75
- w_key: bfloat16 [5120, 1024], P(('unit', 'rows'), 'tp'), parts along dimension 0, may hold values from -0.125 to 0.125
- low_key: bfloat16 [5120, 64], P(('unit', 'rows')), parts along dimension 0, may hold values from -0.125 to 0.125
- high_key: bfloat16 [128, 1024], P('unit', 'tp'), parts along dimension 0, may hold values from -0.75 to 0.75
- w_value: bfloat16 [5120, 1024], P(('unit', 'rows'), 'tp'), parts along dimension 0, may hold values from -0.125 to 0.125
- low_value: bfloat16 [5120, 64], P(('unit', 'rows')), parts along dimension 0, may hold values from -0.125 to 0.125
- high_value: bfloat16 [128, 1024], P('unit', 'tp'), parts along dimension 0, may hold values from -0.75 to 0.75
- w_mixed: bfloat16 [8192, 2560], P(('unit', 'tp'), 'rows'), parts along dimension 0, may hold values from -0.09375 to 0.09375
- low_mixed: bfloat16 [8192, 64], P(('unit', 'tp')), parts along dimension 0, may hold values from -0.09375 to 0.09375
- high_mixed: bfloat16 [128, 2560], P('unit', 'rows'), parts along dimension 0, may hold values from -0.75 to 0.75
- norm_train: float32 [5120], P(('unit', 'rows', 'tp')), parts along dimension 0, may hold values from 0.25 to 1.75
- norm_step: float32 [5120], P(('unit', 'rows', 'tp')), parts along dimension 0, may hold values from -0.3 to 0.3
Outputs:
- final_query: bfloat16 [5120, 4096], P('unit', 'tp'), parts along dimension 0
- final_key: bfloat16 [5120, 1024], P('unit', 'tp'), parts along dimension 0
- final_value: bfloat16 [5120, 1024], P('unit', 'tp'), parts along dimension 0
- final_mixed: bfloat16 [8192, 2560], P(('unit', 'tp')), parts along dimension 0
- serve_norm: bfloat16 [5120], P('unit'), parts along dimension 0
There are 2 independent parts, one for each index of `unit`. A program takes and returns all parts, laid end to end along the dimension named above; each array names one. Nothing has to cross between parts.
All inputs are finite; a program needn't handle non-finite values.
Results may differ from a plain program's by a relative error of at most 0.001.
Values may be sent and summed in bfloat16 or wider, within the bound.
A program may use at most 128 MiB of HBM per device.

v0:
```python
import jax
import jax.numpy as jnp
from jax import lax
from jax.sharding import PartitionSpec as P

mix_rate = 0.5


def shards(
    w_query,
    low_query,
    high_query,
    w_key,
    low_key,
    high_key,
    w_value,
    low_value,
    high_value,
    w_mixed,
    low_mixed,
    high_mixed,
    norm_train,
    norm_step,
):
    result_query = w_query.astype(jnp.float32) + mix_rate * jnp.dot(
        low_query, high_query, preferred_element_type=jnp.float32
    )
    result_key = w_key.astype(jnp.float32) + mix_rate * jnp.dot(
        low_key, high_key, preferred_element_type=jnp.float32
    )
    result_value = w_value.astype(jnp.float32) + mix_rate * jnp.dot(
        low_value, high_value, preferred_element_type=jnp.float32
    )
    result_mixed = w_mixed.astype(jnp.float32) + mix_rate * jnp.dot(
        low_mixed, high_mixed, preferred_element_type=jnp.float32
    )
    narrow_query, narrow_key, narrow_value, narrow_mixed = (
        result_query.astype(jnp.bfloat16),
        result_key.astype(jnp.bfloat16),
        result_value.astype(jnp.bfloat16),
        result_mixed.astype(jnp.bfloat16),
    )
    final_query, final_key, final_value, final_mixed = (
        lax.all_gather(narrow_query, "rows", axis=0, tiled=True),
        lax.all_gather(narrow_key, "rows", axis=0, tiled=True),
        lax.all_gather(narrow_value, "rows", axis=0, tiled=True),
        lax.all_gather(narrow_mixed, "rows", axis=1, tiled=True),
    )
    serve_norm = lax.all_gather(
        (norm_train + norm_step).astype(jnp.bfloat16), ("rows", "tp"), axis=0, tiled=True
    )
    return (final_query, final_key, final_value, final_mixed, serve_norm)


def solution(mesh):
    return jax.shard_map(
        shards,
        mesh=mesh,
        in_specs=(
            P(("unit", "rows"), "tp"),
            P(("unit", "rows"), None),
            P("unit", "tp"),
            P(("unit", "rows"), "tp"),
            P(("unit", "rows"), None),
            P("unit", "tp"),
            P(("unit", "rows"), "tp"),
            P(("unit", "rows"), None),
            P("unit", "tp"),
            P(("unit", "tp"), "rows"),
            P(("unit", "tp"), None),
            P("unit", "rows"),
            P(("unit", "rows", "tp")),
            P(("unit", "rows", "tp")),
        ),
        out_specs=(
            P("unit", "tp"),
            P("unit", "tp"),
            P("unit", "tp"),
            P(("unit", "tp"), None),
            P("unit"),
        ),
        check_vma=False,
    )
```

profile of v0, /device:TPU:0, one launch (start us, length us, event | category | flops | bytes accessed | tf_op | source)
XLA Modules:
  0.0 295.5 jit_solution(12324406735975937253)
XLA Ops:
  7.2 0.0 copy-start
  7.2 0.0 all-gather.7.cloned.1.call-start
  7.2 2.1 fusion.2
  9.4 0.0 all-gather.7.cloned.1.call-update
  9.4 0.0 all-gather.9.cloned.1.call-start
  9.5 2.1 fusion.3
  11.6 0.0 all-gather.9.cloned.1.call-update
  11.7 0.0 all-gather.5.cloned.1.call-start
  11.7 2.5 add_convert_fusion.1
  14.2 0.0 all-gather.5.cloned.1.call-update
  14.2 0.0 all-gather.11.cloned.1.call-start
  14.3 1.6 add_convert_fusion
  15.9 0.0 all-gather.11.cloned.1.call-update
  15.9 0.6 dynamic-slice
  17.2 0.2 dynamic-update-slice
  17.5 46.0 %all-reduce = bf16[2560]{0:T(1024)(128)(2,1)} all-reduce(bf16[2560]{0:T(1024)(128)(2,1)S(1)} %dynamic-update-slice), channel_id=1, replica_groups=mesh['rows'=4,'tp'=4,'unit'=2] {'rows','tp'}, use_global_device_ids=true, to_apply=%add | all-reduce | flops 2560 | bytes 10240
  63.5 16.7 %all-gather.9.cloned.1.call-done = bf16[2560,256]{1,0:T(8,128)(2,1)} async-done(((bf16[640,256]{1,0:T(8,128)(2,1)}), bf16[2560,256]{1,0:T(8,128)(2,1)}) %all-gather.9.cloned.1.call-update) | async-done | bytes 1310736 | tf_op jit(solution)/shard_map/all_gather | solution.py:46
  80.3 99.4 %all-gather.5.cloned.1.call-done = bf16[2560,1024]{1,0:T(8,128)(2,1)} async-done(((bf16[640,1024]{1,0:T(8,128)(2,1)}), bf16[2560,1024]{1,0:T(8,128)(2,1)}) %all-gather.5.cloned.1.call-update) | async-done | bytes 5242896 | tf_op jit(solution)/shard_map/all_gather | solution.py:44
  179.7 98.4 %all-gather.11.cloned.1.call-done = bf16[1024,2560]{1,0:T(8,128)(2,1)} async-done(((bf16[1024,640]{1,0:T(8,128)(2,1)}), bf16[1024,2560]{1,0:T(8,128)(2,1)}) %all-gather.11.cloned.1.call-update) | async-done | bytes 5242896 | tf_op jit(solution)/shard_map/all_gather | solution.py:47
  278.1 5.6 %copy.24 = bf16[2560,1024]{1,0:T(8,128)(2,1)} copy(bf16[2560,1024]{1,0:T(8,128)(2,1)} %all-gather.5.cloned.1.call-done) | data formatting | bytes 10485760
  283.7 1.1 copy.25
  284.8 0.7 copy-done.5
  285.5 1.1 copy.26
  286.6 2.4 copy.27
  (23 shorter events, 0.1 us)
Async XLA Ops:
  7.2 4.5 %copy-start = (bf16[64,1024]{1,0:T(8,128)(2,1)S(1)}, bf16[64,1024]{1,0:T(8,128)(2,1)}, u32[]{:S(2)}) copy-start(bf16[64,1024]{1,0:T(8,128)(2,1)} %param.16) | copy-start | bytes 393220
  7.2 4.5 %copy-start.2 = (bf16[640,1024]{1,0:T(8,128)(2,1)S(1)}, bf16[640,1024]{1,0:T(8,128)(2,1)}, u32[]{:S(2)}) copy-start(bf16[640,1024]{1,0:T(8,128)(2,1)} %param.14) | copy-start | bytes 3932164
  7.2 56.3 %all-gather.7.cloned.1.call-start = ((), (), s32[]{:S(2)}) async-start(), calls=%async_computation.1 | async-start | bytes 1638400 | tf_op jit(solution)/shard_map/all_gather | solution.py:45
  9.4 4.9 %copy-start.3 = (bf16[1024,640]{1,0:T(8,128)(2,1)S(1)}, bf16[1024,640]{1,0:T(8,128)(2,1)}, u32[]{:S(2)}) copy-start(bf16[1024,640]{1,0:T(8,128)(2,1)} %param.23) | copy-start | bytes 3932164
  9.4 4.9 %copy-start.6 = (bf16[1024,64]{0,1:T(8,128)(2,1)S(1)}, bf16[1024,64]{0,1:T(8,128)(2,1)}, u32[]{:S(2)}) copy-start(bf16[1024,64]{0,1:T(8,128)(2,1)} %param.24) | copy-start | bytes 393220
  9.4 4.9 %copy-start.7 = (bf16[64,640]{1,0:T(8,128)(2,1)S(1)}, bf16[64,640]{1,0:T(8,128)(2,1)}, u32[]{:S(2)}) copy-start(bf16[64,640]{1,0:T(8,128)(2,1)} %param.25) | copy-start | bytes 245764
  9.4 70.8 %all-gather.9.cloned.1.call-start = ((), (), s32[]{:S(2)}) async-start(), calls=%async_computation.2 | async-start | bytes 1638400 | tf_op jit(solution)/shard_map/all_gather | solution.py:46
  11.7 168.0 %all-gather.5.cloned.1.call-start = ((), (), s32[]{:S(2)}) async-start(), calls=%async_computation | async-start | bytes 6553600 | tf_op jit(solution)/shard_map/all_gather | solution.py:44
  14.2 1.7 copy-start.10
  14.2 3.0 %copy-start.8 = (f32[160]{0:T(256)S(1)}, f32[160]{0:T(256)}, u32[]{:S(2)}) copy-start(f32[160]{0:T(256)} %param.26) | copy-start | bytes 1924
  14.2 3.0 %copy-start.9 = (f32[160]{0:T(256)S(1)}, f32[160]{0:T(256)}, u32[]{:S(2)}) copy-start(f32[160]{0:T(256)} %param.27) | copy-start | bytes 1924
  14.2 263.9 %all-gather.11.cloned.1.call-start = ((), (), s32[]{:S(2)}) async-start(), calls=%async_computation.3 | async-start | bytes 6553600 | tf_op jit(solution)/shard_map/all_gather | solution.py:47
  63.5 220.2 %copy-start.4 = (bf16[2560,256]{1,0:T(8,128)(2,1)S(1)}, bf16[2560,256]{1,0:T(8,128)(2,1)}, u32[]{:S(2)}) copy-start(bf16[2560,256]{1,0:T(8,128)(2,1)} %all-gather.7.cloned.1.call-done) | copy-start | bytes 3932164
  278.1 8.5 %copy-start.1 = (bf16[1024,2560]{1,0:T(8,128)(2,1)S(1)}, bf16[1024,2560]{1,0:T(8,128)(2,1)}, u32[]{:S(2)}) copy-start(bf16[1024,2560]{1,0:T(8,128)(2,1)} %all-gather.11.cloned.1.call-done) | copy-start | bytes 15728644
  283.7 1.8 copy-start.5
Sparse Core Ops, SparseCore 0:
  10.1 36.3 all-gather.6
  48.7 31.4 all-gather.8
  82.4 97.2 all-gather.4
  181.7 96.3 all-gather.10
where the time goes:
time: 296 us; the launch traced here: 295 us
  waiting for transfers between devices  215 us (73%)
  blocking collectives  46 us (16%)
  between operations  14.5 us (5%)
  local copies, waits for them, and re-layouts  11.7 us (4%)
  matrix products  8.35 us (3%)
    all_gather x1, waiting for transfers between devices, shards(): lax.all_gather(narrow_query, 'rows', axis=0, tiled=True)  99.4 us
    all_gather x1, waiting for transfers between devices, shards(): lax.all_gather(narrow_mixed, 'rows', axis=1, tiled=True)  98.4 us
    unnamed x1, blocking collectives  46 us
    all_gather x1, waiting for transfers between devices, shards(): lax.all_gather(narrow_value, 'rows', axis=0, tiled=True)  16.7 us
    unnamed x29, local copies, waits for them, and re-layouts  11.7 us
  transfers between devices with their start and end apart: 4, of which 3 were waited for; matrix products, arithmetic and copies ran while one was open for 2% of the time, Pallas kernels for 0%

commit v1 on v0

--- a/solution.py
+++ b/solution.py
@@ -44,7 +44,9 @@
         lax.all_gather(narrow_query, "rows", axis=0, tiled=True),
         lax.all_gather(narrow_key, "rows", axis=0, tiled=True),
         lax.all_gather(narrow_value, "rows", axis=0, tiled=True),
-        lax.all_gather(narrow_mixed, "rows", axis=1, tiled=True),
+        jnp.concatenate(
+            lax.all_to_all(jnp.stack([narrow_mixed] * lax.axis_size("rows")), "rows", 0, 0), axis=1
+        ),
     )
     serve_norm = lax.all_gather(
         (norm_train + norm_step).astype(jnp.bfloat16), ("rows", "tp"), axis=0, tiled=True

time: 296 us -> 280 us (0.946)
  waiting for transfers between devices: 215 us -> 57.2 us
  blocking collectives: 46 us -> 166 us
  local copies, waits for them, and re-layouts: 11.7 us -> 27.7 us
  starting transfers between devices: 0.16 us -> 6.6 us
    unnamed x1, blocking collectives: 46 us -> 166 us
    all_gather x1 -> x0, waiting for transfers between devices: 98.4 us -> none  [shards(): lax.all_gather(narrow_mixed, 'rows', axis=1, tiled=True)]
    all_gather x1, waiting for transfers between devices: 99.4 us -> 57.2 us  [shards(): lax.all_gather(narrow_query, 'rows', axis=0, tiled=True)]
    all_gather x1, waiting for transfers between devices: 16.7 us -> 0.01 us  [shards(): lax.all_gather(narrow_value, 'rows', axis=0, tiled=True)]
    all_to_all x0 -> x1, local copies, waits for them, and re-layouts: none -> 7.87 us  [shards(): lax.all_to_all(jnp.stack([narrow_mixed] * lax.axis_size('rows')), 'rows',...]
    all_to_all x0 -> x1, starting transfers between devices: none -> 6.48 us  [shards(): lax.all_to_all(jnp.stack([narrow_mixed] * lax.axis_size('rows')), 'rows',...]
    unnamed x29 -> x25, local copies, waits for them, and re-layouts: 11.7 us -> 17.1 us
  transfers between devices with their start and end apart: 4 -> 4, of which waited for: 3 -> 1; matrix products, arithmetic and copies ran while one was open for 2% -> 9% of each run, Pallas kernels for 0% -> 0%
where the time goes in v1:
time: 280 us
  blocking collectives  166 us (59%)
  waiting for transfers between devices  57.2 us (20%)
  local copies, waits for them, and re-layouts  27.7 us (10%)
  between operations  14.5 us (5%)
  matrix products  7.59 us (3%)
  starting transfers between devices  6.6 us (2%)
    unnamed x1, blocking collectives  166 us
    all_gather x1, waiting for transfers between devices, shards(): lax.all_gather(narrow_query, 'rows', axis=0, tiled=True)  57.2 us
    unnamed x25, local copies, waits for them, and re-layouts  17.1 us
    all_to_all x1, local copies, waits for them, and re-layouts, shards(): lax.all_to_all(jnp.stack([narrow_mixed] * lax.axis_size('rows')), 'rows',...  7.87 us
    all_to_all x1, starting transfers between devices, shards(): lax.all_to_all(jnp.stack([narrow_mixed] * lax.axis_size('rows')), 'rows',...  6.48 us
  transfers between devices with their start and end apart: 4, of which 1 were waited for; matrix products, arithmetic and copies ran while one was open for 9% of the time, Pallas kernels for 0%

profile of v1, /device:TPU:0, one launch (start us, length us, event | category | flops | bytes accessed | tf_op | source)
XLA Modules:
  0.0 279.7 jit_solution(3286545281461018136)
XLA Ops:
  7.2 0.0 copy-start
  7.2 0.0 all-gather.6.cloned.1.call-start
  7.2 2.1 fusion.2
  9.3 0.0 all-gather.6.cloned.1.call-update
  9.3 0.0 all-gather.8.cloned.1.call-start
  9.4 2.0 fusion.3
  11.4 0.0 all-gather.8.cloned.1.call-update
  11.4 1.9 add_convert_fusion
  13.4 2.8 stack.2
  16.1 6.5 %all-to-all-start = ((bf16[4,1024,640]{2,1,0:T(8,128)(2,1)}), bf16[4,1024,640]{2,1,0:T(8,128)(2,1)}, u32[]{:S(2)}, u32[]{:S(2)}) async-start(bf16[4,1024,640]{2,1,0:T(8,128)(2,1)} %stack.2), calls=%async_computation | async-start | bytes 10485760 | tf_op jit(solution)/shard_map/all_to_all | solution.py:48
  22.6 0.0 all-gather.4.cloned.1.call-start
  22.7 1.6 add_convert_fusion.1
  24.3 0.0 all-gather.4.cloned.1.call-update
  24.3 0.6 dynamic-slice
  25.6 0.2 dynamic-update-slice
  25.8 166.1 %all-reduce = bf16[2560]{0:T(1024)(128)(2,1)} all-reduce(bf16[2560]{0:T(1024)(128)(2,1)S(1)} %dynamic-update-slice), channel_id=1, replica_groups=mesh['rows'=4,'tp'=4,'unit'=2] {'rows','tp'}, use_global_device_ids=true, to_apply=%add | all-reduce | flops 2560 | bytes 10240
  192.0 0.0 all-to-all-done
  192.0 7.9 %copy.19 = bf16[4,1024,640]{1,2,0:T(8,128)(2,1)} copy(bf16[4,1024,640]{2,1,0:T(8,128)(2,1)} %all-to-all-done) | data formatting | bytes 10485760 | tf_op jit(solution)/shard_map/all_to_all | solution.py:48
  199.8 7.9 %copy.20 = bf16[1024,2560]{1,0:T(8,128)(2,1)} copy(bf16[1024,2560]{0,1:T(8,128)(2,1)} %bitcast.12) | data formatting | bytes 10485760
  207.8 57.2 %all-gather.4.cloned.1.call-done = bf16[2560,1024]{1,0:T(8,128)(2,1)} async-done(((bf16[640,1024]{1,0:T(8,128)(2,1)}), bf16[2560,1024]{1,0:T(8,128)(2,1)}) %all-gather.4.cloned.1.call-update) | async-done | bytes 5242896 | tf_op jit(solution)/shard_map/all_gather | solution.py:44
  264.9 5.4 %copy.25 = bf16[2560,1024]{1,0:T(8,128)(2,1)} copy(bf16[2560,1024]{1,0:T(8,128)(2,1)} %all-gather.4.cloned.1.call-done) | data formatting | bytes 10485760
  270.4 1.1 copy.26
  271.4 0.7 copy-done.3
  272.2 1.1 copy.27
  (20 shorter events, 0.0 us)
Async XLA Ops:
  7.2 4.3 %copy-start = (bf16[1024,64]{0,1:T(8,128)(2,1)S(1)}, bf16[1024,64]{0,1:T(8,128)(2,1)}, u32[]{:S(2)}) copy-start(bf16[1024,64]{0,1:T(8,128)(2,1)} %param.24) | copy-start | bytes 393220
  7.2 184.8 %all-gather.6.cloned.1.call-start = ((), (), s32[]{:S(2)}) async-start(), calls=%async_computation.2 | async-start | bytes 1638400 | tf_op jit(solution)/shard_map/all_gather | solution.py:45
  9.3 182.7 %all-gather.8.cloned.1.call-start = ((), (), s32[]{:S(2)}) async-start(), calls=%async_computation.3 | async-start | bytes 1638400 | tf_op jit(solution)/shard_map/all_gather | solution.py:46
  16.1 6.5 %copy-start.1 = (bf16[640,1024]{1,0:T(8,128)(2,1)S(1)}, bf16[640,1024]{1,0:T(8,128)(2,1)}, u32[]{:S(2)}) copy-start(bf16[640,1024]{1,0:T(8,128)(2,1)} %param.14) | copy-start | bytes 3932164
  16.1 6.6 %copy-start.4 = (bf16[64,1024]{1,0:T(8,128)(2,1)S(1)}, bf16[64,1024]{1,0:T(8,128)(2,1)}, u32[]{:S(2)}) copy-start(bf16[64,1024]{1,0:T(8,128)(2,1)} %param.16) | copy-start | bytes 393220
  16.1 6.6 %copy-start.5 = (bf16[640,64]{0,1:T(8,128)(2,1)S(1)}, bf16[640,64]{0,1:T(8,128)(2,1)}, u32[]{:S(2)}) copy-start(bf16[640,64]{0,1:T(8,128)(2,1)} %param.15) | copy-start | bytes 245764
  16.1 175.9 %all-to-all-start = ((bf16[4,1024,640]{2,1,0:T(8,128)(2,1)}), bf16[4,1024,640]{2,1,0:T(8,128)(2,1)}, u32[]{:S(2)}, u32[]{:S(2)}) async-start(bf16[4,1024,640]{2,1,0:T(8,128)(2,1)} %stack.2), calls=%async_computation | async-start | bytes 10485760 | tf_op jit(solution)/shard_map/all_to_all | solution.py:48
  22.6 1.7 copy-start.8
  22.6 2.9 %copy-start.6 = (f32[160]{0:T(256)S(1)}, f32[160]{0:T(256)}, u32[]{:S(2)}) copy-start(f32[160]{0:T(256)} %param.26) | copy-start | bytes 1924
  22.6 3.0 %copy-start.7 = (f32[160]{0:T(256)S(1)}, f32[160]{0:T(256)}, u32[]{:S(2)}) copy-start(f32[160]{0:T(256)} %param.27) | copy-start | bytes 1924
  22.6 242.3 %all-gather.4.cloned.1.call-start = ((), (), s32[]{:S(2)}) async-start(), calls=%async_computation.1 | async-start | bytes 6553600 | tf_op jit(solution)/shard_map/all_gather | solution.py:44
  207.8 62.6 %copy-start.2 = (bf16[2560,256]{1,0:T(8,128)(2,1)S(1)}, bf16[2560,256]{1,0:T(8,128)(2,1)}, u32[]{:S(2)}) copy-start(bf16[2560,256]{1,0:T(8,128)(2,1)} %all-gather.6.cloned.1.call-done) | copy-start | bytes 3932164
  270.4 1.8 copy-start.3
Sparse Core Ops, SparseCore 0:
  10.1 72.9 all-gather.5
  85.3 68.6 all-gather.7
  156.2 108.7 all-gather.3
